TPU v7x, 32 devices: a whole 2x2x4 slice. The times are simulated.
32 devices in a mesh: wide: 16 (over z, y, core), narrow: 2 (over x).
Axes of the slice: x: 2, y: 2, z: 4, core: 2. Of those that a mesh axis runs over, the one named last changes fastest.
Arguments:
- src_field: bfloat16 [2, 16, 65536], P(None, 'narrow', 'wide'), may hold values from -6 to 6
- src_depth: int32 [65536], P(('wide', 'narrow')), may hold values from 0 to 16, as said below
- packed_counts: int32 [4096, 64, 128], P(('wide', 'narrow')), may hold values from 0 to 100664832, as said below
- pair_source: int32 [4096], P(('wide', 'narrow')), may hold values from 0 to 15
- pair_home: int32 [4096], P(('wide', 'narrow')), may hold values from 0 to 1023, as said below
- pair_count: int32 [32], P(('wide', 'narrow')), may hold values from 64 to 128, as said below
Outputs:
- remapped: bfloat16 [2, 16, 131072], P(None, 'narrow', 'wide')
Inputs may be any that keep to these rules, and one draw needn't show every extreme that they name: `src_depth`: depth 0 marks a dry source cell. `packed_counts`: word (p, i, j) holds count (p, i, j) plus 65536 times count (p, i + 64, j); every count lies between 0 and 1536. The target block pair_home[p] is held by wide index pair_home[p] // 64, which differs by at most 2, counted cyclically over the wide axis, from the wide index of the device that holds pair p. Among the 128 pairs of one device at most 51 have target blocks on one wide index, and on some wide index exactly 51 live pairs of that device. A device's pairs from position pair_count[d] on are padding; some device has all 128 live.
All inputs are finite; a program needn't handle non-finite values.
Results may differ from a plain program's by a relative error of at most 0.0054.
Values may be sent and summed in bfloat16 or wider, within the bound.
A program may use at most 64 MiB of HBM per device.

v0:
```python
import jax
import jax.numpy as jnp
from jax import lax
from jax.sharding import PartitionSpec as P

DENOM = 256
REACH = 2
TB_DEV = 64
wet_limit = 0.001


def passed_along(block, axis, distance):
    devices = range(lax.axis_size(axis))
    route = [((i - distance) % len(devices), i) for i in devices]
    return lax.ppermute(block, axis, route)


def unpack_counts(packed_words):
    return jnp.concatenate([packed_words % 65536, packed_words // 65536], axis=-2)


def block_sums(targets, received, block_count):
    owners = jnp.arange(block_count, dtype=jnp.int32)
    select = (targets[:, None] == owners[None, :]).astype(jnp.bfloat16)
    return jnp.einsum("rq,rlcb->lcqb", select, received, preferred_element_type=jnp.float32)


def per_device(src_field, src_depth, packed_counts, pair_source, pair_home, pair_count):
    narrow_size = lax.axis_size("narrow")
    wide_size = lax.axis_size("wide")
    field_vars = src_field.shape[0]
    components = field_vars + 1
    block_cells = packed_counts.shape[2]
    own_cells = src_depth.shape[0]
    own_tiles = own_cells // block_cells
    pair_slots = pair_source.shape[0]
    offset_count = 2 * REACH + 1
    capacity = max(2, 2 * pair_slots // offset_count)
    own_field = lax.all_to_all(src_field, "narrow", split_axis=2, concat_axis=1, tiled=True)
    levels = own_field.shape[1]
    part_levels = levels // narrow_size
    level_ids = jnp.arange(levels, dtype=jnp.int32)
    wet_levels = level_ids[:, None] < src_depth[None, :]
    masked = jnp.where(wet_levels[None, :, :], own_field, jnp.zeros_like(own_field))
    stacked = jnp.concatenate(
        [jnp.transpose(masked, (1, 0, 2)), wet_levels.astype(jnp.bfloat16)[:, None, :]], axis=1
    )
    by_tile = jnp.transpose(stacked.reshape(levels * components, own_tiles, block_cells), (1, 0, 2))
    picked = jnp.take(by_tile, pair_source, axis=0)
    weight = (unpack_counts(packed_counts).astype(jnp.float32) / DENOM).astype(jnp.bfloat16)
    pair_terms = lax.dot_general(
        picked, weight, (((2,), (2,)), ((0,), (0,))), preferred_element_type=jnp.float32
    )
    pair_terms = pair_terms.astype(jnp.bfloat16)
    is_live = jnp.arange(pair_slots, dtype=jnp.int32) < pair_count[0]
    wide_index = lax.axis_index("wide")
    destination = pair_home // TB_DEV
    local_block = pair_home % TB_DEV
    offset_index = (destination - wide_index + REACH + wide_size) % wide_size
    bound_for = (
        (offset_index[:, None] == jnp.arange(offset_count, dtype=jnp.int32)[None, :])
        & is_live[:, None]
    ).astype(jnp.int32)
    before = jnp.cumsum(bound_for, axis=0) - bound_for
    position = jnp.sum(before * bound_for, axis=1)
    slot_index = jnp.where(is_live, offset_index * capacity + position, offset_count * capacity)
    outgoing = (
        jnp.zeros((offset_count * capacity, levels * components, block_cells), jnp.bfloat16)
        .at[slot_index]
        .set(pair_terms, mode="drop")
    )
    targets = (
        jnp.full((offset_count * capacity,), TB_DEV, jnp.int32)
        .at[slot_index]
        .set(local_block, mode="drop")
    )
    outgoing = outgoing.reshape(offset_count, capacity, levels, components, block_cells)
    targets = targets.reshape(offset_count, capacity)
    shift_list = [shift_by for shift_by in range(-REACH, REACH + 1) if shift_by != 0]
    partial_value = block_sums(targets[REACH], outgoing[REACH], TB_DEV)
    for shift_by in shift_list:
        moved_terms, moved_owners = passed_along(
            (outgoing[REACH + shift_by], targets[REACH + shift_by]), "wide", shift_by
        )
        partial_value = partial_value + block_sums(moved_owners, moved_terms, TB_DEV)
    block_totals = lax.psum_scatter(partial_value, "narrow", scatter_dimension=0, tiled=True)
    numerators = block_totals[:, :field_vars]
    wet_total = block_totals[:, field_vars]
    covered = wet_total > wet_limit
    safe_wet = jnp.where(covered, wet_total, jnp.ones_like(wet_total))
    result = jnp.where(covered[:, None], numerators / safe_wet[:, None], jnp.zeros_like(numerators))
    result = jnp.transpose(result, (1, 0, 2, 3)).reshape(
        field_vars, part_levels, TB_DEV * block_cells
    )
    return result.astype(jnp.bfloat16)


def solution(mesh):
    placed = (
        P(None, "narrow", "wide"),
        P(("wide", "narrow")),
        P(("wide", "narrow"), None, None),
        P(("wide", "narrow")),
        P(("wide", "narrow")),
        P(("wide", "narrow")),
    )
    return jax.shard_map(
        per_device, mesh=mesh, in_specs=placed, out_specs=P(None, "narrow", "wide"), check_vma=False
    )
```

profile of v0, /device:TPU:0, one launch (start us, length us, event | category | flops | bytes accessed | tf_op | source)
XLA Modules:
  0.0 141.5 jit_solution(15521793403621437424)
XLA Ops:
  6.5 4.4 %copy.29 = bf16[2,8,4096]{1,0,2:T(2,128)(2,1)S(1)} copy(bf16[2,8,4096]{2,1,0:T(8,128)(2,1)} %param.6) | data formatting | bytes 262144 | tf_op args[0]
  10.9 2.8 %reshape.126 = bf16[2,2,16384]{2,1,0:T(2,128)(2,1)} reshape(bf16[4096,2,8]{2,1,0:T(2,128)(2,1)S(1)} %bitcast.60) | data formatting | bytes 262144
  13.8 4.2 %all-to-all-start = ((bf16[2,2,16384]{2,1,0:T(2,128)(2,1)}), bf16[2,2,16384]{2,1,0:T(2,128)(2,1)S(1)}, u32[]{:S(2)}, u32[]{:S(2)}) async-start(bf16[2,2,16384]{2,1,0:T(2,128)(2,1)} %reshape.126), calls=%async_computation | async-start | bytes 262144 | tf_op jit(solution)/shard_map/all_to_all | solution.py:39
  18.0 0.1 compare_convert_fusion
  18.9 0.1 fusion.29
  19.0 0.2 reduce_window_sum.11
  19.2 0.2 select_reduce_fusion
  19.4 7.1 %add_select_fusion.1 = (s32[128,64,128]{2,1,0:T(8,128)}, s32[128,64,128]{2,1,0:T(8,128)}) fusion(s32[128,64,128]{2,1,0:T(8,128)} %param.8), kind=kLoop, calls=%fused_computation.8 | loop fusion | flops 19922944 | bytes 12582912 | tf_op jit(solution)/shard_map/jit(remainder)/select_n | solution.py:19
  26.5 2.5 %reshape.127 = bf16[4096,2,8]{2,1,0:T(2,128)(2,1)S(1)} reshape(bf16[2,2,16384]{2,1,0:T(2,128)(2,1)S(1)} %all-to-all-done) | data formatting | bytes 262144
  28.9 1.4 copy.30
  30.3 0.2 fusion.27
  30.6 0.3 pad_maximum_fusion
  30.9 0.2 reshape.91
  31.1 0.9 gather_fusion
  32.0 7.7 %fusion.7 = bf16[128,48,128]{2,1,0:T(8,128)(2,1)} fusion(s32[128,64,128]{2,1,0:T(8,128)} %get-tuple-element.6, s32[128,64,128]{2,1,0:T(8,128)} %get-tuple-element.5, bf16[128,48,128]{2,1,0:T(8,128)(2,1)S(1)} %gather_fusion, pred[128]{0:T(512)(128)(4,1)S(1)} %compare_and_fusion), kind=kOutput, calls=%fused_computation.16 | convolution fusion | flops 211288064 | bytes 11534464 | tf_op jit(solution)/shard_map/dot_general | solution.py:51
  39.8 0.4 broadcast_in_dim.71
  40.2 11.8 %scatter_fusion = bf16[255,48,128]{2,1,0:T(8,128)(2,1)S(1)} fusion(bf16[255,48,128]{2,1,0:T(8,128)(2,1)S(1)} %broadcast_in_dim.71, s32[128]{0:T(128)S(1)} %compare_select_fusion.2, bf16[128,48,128]{2,1,0:T(8,128)(2,1)} %fusion.7), kind=kCustom, calls=%fused_computation.1 | custom fusion | bytes 4719104 | tf_op jit(solution)/shard_map/scatter | solution.py:70
  52.0 1.7 %fusion.52 = (bf16[51,48,128]{2,1,0:T(8,128)(2,1)}, bf16[51,48,128]{2,1,0:T(8,128)(2,1)}, bf16[51,48,128]{2,1,0:T(8,128)(2,1)S(1)}, bf16[51,48,128]{2,1,0:T(8,128)(2,1)}, bf16[51,48,128]{2,1,0:T(8,128)(2,1)}) fusion(bf16[255,48,128]{2,1,0:T(8,128)(2,1)S(1)} %scatter_fusion), kind=kLoop, calls=%fused_computation.81 | loop fusion | bytes 6266880 | tf_op jit(solution)/shard_map/slice | solution.py:83
  53.7 0.2 copy.36
  53.9 0.1 copy.37
  54.0 4.6 %collective-permute-start.2 = (bf16[51,16,3,128]{3,1,2,0:T(8,128)(2,1)S(1)}, bf16[51,16,3,128]{3,1,2,0:T(8,128)(2,1)S(1)}, u32[]{:S(2)}, u32[]{:S(2)}) collective-permute-start(bf16[51,16,3,128]{3,1,2,0:T(8,128)(2,1)S(1)} %copy.37), channel_id=1, source_target_pairs={{2,0},{4,2},{6,4},{8,6},{10,8},{12,10},{14,12},{16,14},{18,16},{20... | collective-permute-start | bytes 1880072 | tf_op jit(solution)/shard_map/ppermute | solution.py:15
  58.6 1.0 scatter_custom_fusion.1
  59.6 1.2 copy.33
  60.9 0.1 copy.34
  61.0 0.7 collective-permute-start
  61.7 0.1 fusion.53
  61.7 0.3 collective-permute-start.3
  62.0 1.4 collective-permute-start.1
  63.4 0.2 copy.39
  63.6 0.1 copy.40
  63.7 0.2 collective-permute-start.4
  64.0 0.2 copy.32
  64.1 0.5 fusion.31
  64.6 0.2 copy.42
  64.8 0.1 copy.43
  64.9 15.0 %collective-permute-done.3 = s32[51]{0:T(128)S(1)} collective-permute-done((s32[51]{0:T(128)S(1)}, s32[51]{0:T(128)S(1)}, u32[]{:S(2)}, u32[]{:S(2)}) %collective-permute-start.3) | collective-permute-done | bytes 236 | tf_op jit(solution)/shard_map/ppermute | solution.py:15
  79.9 4.8 %collective-permute-start.5 = (s32[51]{0:T(128)S(1)}, s32[51]{0:T(128)S(1)}, u32[]{:S(2)}, u32[]{:S(2)}) collective-permute-start(s32[51]{0:T(128)S(1)} %get-tuple-element.13), channel_id=1, source_target_pairs={{30,0},{0,2},{2,4},{4,6},{6,8},{8,10},{10,12},{12,14},{14,16},{16,... | collective-permute-start | bytes 620 | tf_op jit(solution)/shard_map/ppermute | solution.py:15
  84.7 0.5 fusion.19
  85.2 3.1 %collective-permute-start.7 = (s32[51]{0:T(128)S(1)}, s32[51]{0:T(128)S(1)}, u32[]{:S(2)}, u32[]{:S(2)}) collective-permute-start(s32[51]{0:T(128)S(1)} %get-tuple-element.12), channel_id=1, source_target_pairs={{28,0},{30,2},{0,4},{2,6},{4,8},{6,10},{8,12},{10,14},{12,16},{14,... | collective-permute-start | bytes 620 | tf_op jit(solution)/shard_map/ppermute | solution.py:15
  88.3 0.5 fusion.21
  88.8 0.5 fusion.17
  89.3 14.2 %collective-permute-done.7 = s32[51]{0:T(128)S(1)} collective-permute-done((s32[51]{0:T(128)S(1)}, s32[51]{0:T(128)S(1)}, u32[]{:S(2)}, u32[]{:S(2)}) %collective-permute-start.7) | collective-permute-done | bytes 236 | tf_op jit(solution)/shard_map/ppermute | solution.py:15
  103.5 1.9 %add_bitcast_fusion = f32[16,3,64,128]{3,2,1,0:T(8,128)} fusion(f32[16,3,128,64]{2,3,1,0:T(8,128)S(1)} %fusion.17, f32[16,3,128,64]{2,3,1,0:T(8,128)S(1)} %fusion.19, f32[16,3,128,64]{2,3,1,0:T(8,128)S(1)} %fusion.31, f32[16,3,128,64]{2,3,1,0:T(8,128)S(1)} %fusion.21, bf16[51,16,3,128]{3,1,2,0:T(8,128)(2,1)S(1)} %collective-permute-done.6, ...), kind=kOutput, calls=%fused_computation.17 | convolution fusion | flops 41684160 | bytes 8491212 | tf_op jit(solution)/shard_map/rq,rlcb->lcqb/dot_general | solution.py:25
  105.4 25.3 %reduce-scatter.2.cloned.1.call-done = f32[8,3,64,128]{3,2,1,0:T(8,128)} async-done(((f32[16,3,64,128]{3,2,1,0:T(8,128)}), f32[8,3,64,128]{3,2,1,0:T(8,128)}) %reduce-scatter.2.cloned.1.call-update) | async-done | bytes 786448 | tf_op jit(solution)/shard_map/reduce_scatter | solution.py:86
  130.6 1.0 fusion.25
  131.6 1.0 compare_bitcast_fusion
  132.6 1.1 fusion.26
  133.8 0.9 copy.45
  (31 shorter events, 0.3 us)
Async XLA Ops:
  6.5 11.5 %copy-start.3 = (s32[2048]{0:T(1024)S(1)}, s32[2048]{0:T(1024)}, u32[]{:S(2)}) copy-start(s32[2048]{0:T(1024)} %param.7) | copy-start | bytes 24580
  6.5 11.6 %copy-start.5 = (s32[128]{0:T(128)S(1)}, s32[128]{0:T(128)}, u32[]{:S(2)}) copy-start(s32[128]{0:T(128)} %param.9) | copy-start | bytes 1540
  6.5 12.3 %copy-start.4 = (s32[128]{0:T(128)S(1)}, s32[128]{0:T(128)}, u32[]{:S(2)}) copy-start(s32[128]{0:T(128)} %param.10) | copy-start | bytes 1540
  13.8 12.7 %all-to-all-start = ((bf16[2,2,16384]{2,1,0:T(2,128)(2,1)}), bf16[2,2,16384]{2,1,0:T(2,128)(2,1)S(1)}, u32[]{:S(2)}, u32[]{:S(2)}) async-start(bf16[2,2,16384]{2,1,0:T(2,128)(2,1)} %reshape.126), calls=%async_computation | async-start | bytes 262144 | tf_op jit(solution)/shard_map/all_to_all | solution.py:39
  18.0 112.6 %reduce-scatter.2.cloned.1.call-start = ((), (), s32[]{:S(2)}) async-start(), calls=%async_computation.2 | async-start | bytes 2359296 | tf_op jit(solution)/shard_map/reduce_scatter | solution.py:86
  53.7 9.7 %copy-start.2 = (bf16[51,48,128]{2,1,0:T(8,128)(2,1)S(1)}, bf16[51,48,128]{2,1,0:T(8,128)(2,1)}, u32[]{:S(2)}) copy-start(bf16[51,48,128]{2,1,0:T(8,128)(2,1)} %get-tuple-element.8) | copy-start | bytes 1880068
  53.9 10.1 %copy-start.1 = (bf16[51,48,128]{2,1,0:T(8,128)(2,1)S(1)}, bf16[51,48,128]{2,1,0:T(8,128)(2,1)}, u32[]{:S(2)}) copy-start(bf16[51,48,128]{2,1,0:T(8,128)(2,1)} %get-tuple-element.11) | copy-start | bytes 1880068
  54.0 30.7 %collective-permute-start.2 = (bf16[51,16,3,128]{3,1,2,0:T(8,128)(2,1)S(1)}, bf16[51,16,3,128]{3,1,2,0:T(8,128)(2,1)S(1)}, u32[]{:S(2)}, u32[]{:S(2)}) collective-permute-start(bf16[51,16,3,128]{3,1,2,0:T(8,128)(2,1)S(1)} %copy.37), channel_id=1, source_target_pairs={{2,0},{4,2},{6,4},{8,6},{10,8},{12,10},{14,12},{16,14},{18,16},{20... | collective-permute-start | bytes 1880072 | tf_op jit(solution)/shard_map/ppermute | solution.py:15
  61.0 3.7 %copy-start = (bf16[51,48,128]{2,1,0:T(8,128)(2,1)S(1)}, bf16[51,48,128]{2,1,0:T(8,128)(2,1)}, u32[]{:S(2)}) copy-start(bf16[51,48,128]{2,1,0:T(8,128)(2,1)} %get-tuple-element.7) | copy-start | bytes 1880068
  61.0 27.4 %collective-permute-start = (bf16[51,16,3,128]{3,1,2,0:T(8,128)(2,1)S(1)}, bf16[51,16,3,128]{3,1,2,0:T(8,128)(2,1)S(1)}, u32[]{:S(2)}, u32[]{:S(2)}) collective-permute-start(bf16[51,16,3,128]{3,1,2,0:T(8,128)(2,1)S(1)} %copy.34), channel_id=1, source_target_pairs={{4,0},{6,2},{8,4},{10,6},{12,8},{14,10},{16,12},{18,14},{20,16},{2... | collective-permute-start | bytes 1880072 | tf_op jit(solution)/shard_map/ppermute | solution.py:15
  61.7 18.2 %collective-permute-start.3 = (s32[51]{0:T(128)S(1)}, s32[51]{0:T(128)S(1)}, u32[]{:S(2)}, u32[]{:S(2)}) collective-permute-start(s32[51]{0:T(128)S(1)} %get-tuple-element.14), channel_id=1, source_target_pairs={{2,0},{4,2},{6,4},{8,6},{10,8},{12,10},{14,12},{16,14},{18,16},{20... | collective-permute-start | bytes 620 | tf_op jit(solution)/shard_map/ppermute | solution.py:15
  62.0 23.1 %collective-permute-start.1 = (s32[51]{0:T(128)S(1)}, s32[51]{0:T(128)S(1)}, u32[]{:S(2)}, u32[]{:S(2)}) collective-permute-start(s32[51]{0:T(128)S(1)} %get-tuple-element.15), channel_id=1, source_target_pairs={{4,0},{6,2},{8,4},{10,6},{12,8},{14,10},{16,12},{18,14},{20,16},{2... | collective-permute-start | bytes 620 | tf_op jit(solution)/shard_map/ppermute | solution.py:15
  63.7 25.1 %collective-permute-start.4 = (bf16[51,16,3,128]{3,1,2,0:T(8,128)(2,1)S(1)}, bf16[51,16,3,128]{3,1,2,0:T(8,128)(2,1)S(1)}, u32[]{:S(2)}, u32[]{:S(2)}) collective-permute-start(bf16[51,16,3,128]{3,1,2,0:T(8,128)(2,1)S(1)} %copy.40), channel_id=1, source_target_pairs={{30,0},{0,2},{2,4},{4,6},{6,8},{8,10},{10,12},{12,14},{14,16},{16,... | collective-permute-start | bytes 1880072 | tf_op jit(solution)/shard_map/ppermute | solution.py:15
  79.9 8.9 %collective-permute-start.5 = (s32[51]{0:T(128)S(1)}, s32[51]{0:T(128)S(1)}, u32[]{:S(2)}, u32[]{:S(2)}) collective-permute-start(s32[51]{0:T(128)S(1)} %get-tuple-element.13), channel_id=1, source_target_pairs={{30,0},{0,2},{2,4},{4,6},{6,8},{8,10},{10,12},{12,14},{14,16},{16,... | collective-permute-start | bytes 620 | tf_op jit(solution)/shard_map/ppermute | solution.py:15
  84.7 18.8 %collective-permute-start.6 = (bf16[51,16,3,128]{3,1,2,0:T(8,128)(2,1)S(1)}, bf16[51,16,3,128]{3,1,2,0:T(8,128)(2,1)S(1)}, u32[]{:S(2)}, u32[]{:S(2)}) collective-permute-start(bf16[51,16,3,128]{3,1,2,0:T(8,128)(2,1)S(1)} %copy.43), channel_id=1, source_target_pairs={{28,0},{30,2},{0,4},{2,6},{4,8},{6,10},{8,12},{10,14},{12,16},{14,... | collective-permute-start | bytes 1880072 | tf_op jit(solution)/shard_map/ppermute | solution.py:15
  85.2 18.3 %collective-permute-start.7 = (s32[51]{0:T(128)S(1)}, s32[51]{0:T(128)S(1)}, u32[]{:S(2)}, u32[]{:S(2)}) collective-permute-start(s32[51]{0:T(128)S(1)} %get-tuple-element.12), channel_id=1, source_target_pairs={{28,0},{30,2},{0,4},{2,6},{4,8},{6,10},{8,12},{10,14},{12,16},{14,... | collective-permute-start | bytes 620 | tf_op jit(solution)/shard_map/ppermute | solution.py:15
Sparse Core Ops, SparseCore 0:
  105.5 25.0 reduce-scatter.1
where the time goes:
time: 142 us
  waiting for transfers between devices  54.5 us (38%)
  local copies, waits for them, and re-layouts  30.4 us (21%)
  starting transfers between devices  19.4 us (14%)
  between operations  14.4 us (10%)
  matrix products  11.5 us (8%)
  other arithmetic  11.4 us (8%)
    ppermute x8, waiting for transfers between devices, passed_along(): return lax.ppermute(block, axis, route)  29.2 us
    reduce_scatter x1, waiting for transfers between devices, per_device(): lax.psum_scatter(partial_value, 'narrow', scatter_dimension=0, tiled=True)  25.3 us
    ppermute x8, starting transfers between devices, passed_along(): return lax.ppermute(block, axis, route)  15.2 us
    scatter x1, local copies, waits for them, and re-layouts, per_device(): outgoing = jnp.zeros((offset_count * capacity, levels * components, block...  11.8 us
    unnamed x15, local copies, waits for them, and re-layouts  9.68 us
    dot_general x1, matrix products, per_device(): lax.dot_general(picked, weight, (((2,), (2,)), ((0,), (0,))), preferred_e...  7.73 us
    select_n x1, other arithmetic, unpack_counts(): packed_words % 65536  7.1 us
    all_to_all x1, starting transfers between devices, per_device(): lax.all_to_all(src_field, 'narrow', split_axis=2, concat_axis=1, tiled=True)  4.23 us
  transfers between devices with their start and end apart: 10, of which 3 were waited for; matrix products, arithmetic and copies ran while one was open for 9% of the time, Pallas kernels for 0%

commit v1 on v0

--- a/solution.py
+++ b/solution.py
@@ -7,6 +7,15 @@
 REACH = 2
 TB_DEV = 64
 wet_limit = 0.001
+
+
+def fill_ranges(xin):
+    return jnp.concatenate(
+        lax.all_to_all(
+            jnp.stack(jnp.split(xin, lax.axis_size("narrow"), axis=2), axis=0), "narrow", 0, 0
+        ),
+        1,
+    )
 
 
 def passed_along(block, axis, distance):
@@ -36,7 +45,7 @@
     pair_slots = pair_source.shape[0]
     offset_count = 2 * REACH + 1
     capacity = max(2, 2 * pair_slots // offset_count)
-    own_field = lax.all_to_all(src_field, "narrow", split_axis=2, concat_axis=1, tiled=True)
+    own_field = fill_ranges(src_field)
     levels = own_field.shape[1]
     part_levels = levels // narrow_size
     level_ids = jnp.arange(levels, dtype=jnp.int32)

time: 142 us -> 136 us (0.958)
  local copies, waits for them, and re-layouts: 30.4 us -> 20.4 us
  other arithmetic: 11.4 us -> 14.8 us
    unnamed x15 -> x6, local copies, waits for them, and re-layouts: 9.68 us -> 0.01 us
  transfers between devices with their start and end apart: 10 -> 10, of which waited for: 3 -> 3; matrix products, arithmetic and copies ran while one was open for 9% -> 12% of each run, Pallas kernels for 0% -> 0%
where the time goes in v1:
time: 136 us; the launch traced here: 135 us
  waiting for transfers between devices  54.7 us (40%)
  local copies, waits for them, and re-layouts  20.4 us (15%)
  starting transfers between devices  19.2 us (14%)
  other arithmetic  14.8 us (11%)
  between operations  14.3 us (11%)
  matrix products  11.5 us (8%)
    ppermute x8, waiting for transfers between devices, passed_along(): return lax.ppermute(block, axis, route)  29.4 us
    reduce_scatter x1, waiting for transfers between devices, per_device(): lax.psum_scatter(partial_value, 'narrow', scatter_dimension=0, tiled=True)  25.3 us
    ppermute x8, starting transfers between devices, passed_along(): return lax.ppermute(block, axis, route)  15 us
    scatter x1, local copies, waits for them, and re-layouts, per_device(): outgoing = jnp.zeros((offset_count * capacity, levels * components, block...  11.8 us
    dot_general x1, matrix products, per_device(): lax.dot_general(picked, weight, (((2,), (2,)), ((0,), (0,))), preferred_e...  7.75 us
    select_n x1, other arithmetic, unpack_counts(): packed_words % 65536  7.11 us
    all_to_all x1, starting transfers between devices, fill_ranges(): lax.all_to_all(jnp.stack(jnp.split(xin, lax.axis_size('narrow'), axis=2),...  4.23 us
    dot_general x5, matrix products, block_sums(): jnp.einsum('rq,rlcb->lcqb', select, received, preferred_element_type=jnp....  3.78 us
  transfers between devices with their start and end apart: 10, of which 3 were waited for; matrix products, arithmetic and copies ran while one was open for 12% of the time, Pallas kernels for 0%

profile of v1, /device:TPU:0, one launch (start us, length us, event | category | flops | bytes accessed | tf_op | source)
XLA Modules:
  0.0 134.9 jit_solution(16890409283662385175)
XLA Ops:
  6.5 0.9 slice_bitcast_fusion.1
  7.4 0.7 pad_maximum_fusion.1
  8.1 4.2 %all-to-all-start = ((bf16[2,2,8,2048]{3,2,1,0:T(8,128)(2,1)}), bf16[2,2,8,2048]{3,2,1,0:T(8,128)(2,1)S(1)}, u32[]{:S(2)}, u32[]{:S(2)}) async-start(bf16[2,2,8,2048]{3,2,1,0:T(8,128)(2,1)} %pad_maximum_fusion.1), calls=%async_computation | async-start | bytes 262144 | tf_op jit(solution)/shard_map/all_to_all | solution.py:14
  12.3 0.7 iota_compare_fusion.1
  13.0 0.7 fusion.28
  13.8 0.7 compare_select_fusion.1
  14.4 0.7 compare_and_fusion
  15.8 0.7 and_select_fusion
  16.4 0.1 fusion.30
  16.5 0.2 reduce_window_sum.11
  16.7 0.2 select_reduce_fusion
  16.9 7.1 %add_select_fusion.1 = (s32[128,64,128]{2,1,0:T(8,128)}, s32[128,64,128]{2,1,0:T(8,128)}) fusion(s32[128,64,128]{2,1,0:T(8,128)} %param.8), kind=kLoop, calls=%fused_computation.8 | loop fusion | flops 19922944 | bytes 12582912 | tf_op jit(solution)/shard_map/jit(remainder)/select_n | solution.py:28
  24.1 0.2 copy.30
  24.2 0.2 reshape.99
  24.5 0.9 gather_fusion
  25.4 7.7 %fusion.7 = bf16[128,48,128]{2,1,0:T(8,128)(2,1)} fusion(s32[128,64,128]{2,1,0:T(8,128)} %get-tuple-element.6, s32[128,64,128]{2,1,0:T(8,128)} %get-tuple-element.5, bf16[128,48,128]{2,1,0:T(8,128)(2,1)S(1)} %gather_fusion, pred[128]{0:T(512)(128)(4,1)S(1)} %compare_and_fusion), kind=kOutput, calls=%fused_computation.16 | convolution fusion | flops 211288064 | bytes 11534464 | tf_op jit(solution)/shard_map/dot_general | solution.py:60
  33.1 0.4 broadcast_in_dim.71
  33.6 11.8 %scatter_fusion = bf16[255,48,128]{2,1,0:T(8,128)(2,1)S(1)} fusion(bf16[255,48,128]{2,1,0:T(8,128)(2,1)S(1)} %broadcast_in_dim.71, s32[128]{0:T(128)S(1)} %compare_select_fusion.2, bf16[128,48,128]{2,1,0:T(8,128)(2,1)} %fusion.7), kind=kCustom, calls=%fused_computation.1 | custom fusion | bytes 4719104 | tf_op jit(solution)/shard_map/scatter | solution.py:79
  45.4 1.7 %fusion.53 = (bf16[51,48,128]{2,1,0:T(8,128)(2,1)}, bf16[51,48,128]{2,1,0:T(8,128)(2,1)}, bf16[51,48,128]{2,1,0:T(8,128)(2,1)S(1)}, bf16[51,48,128]{2,1,0:T(8,128)(2,1)}, bf16[51,48,128]{2,1,0:T(8,128)(2,1)}) fusion(bf16[255,48,128]{2,1,0:T(8,128)(2,1)S(1)} %scatter_fusion), kind=kLoop, calls=%fused_computation.85 | loop fusion | bytes 6266880 | tf_op jit(solution)/shard_map/slice | solution.py:92
  47.1 0.2 copy.36
  47.3 0.1 copy.37
  47.4 4.6 %collective-permute-start.2 = (bf16[51,16,3,128]{3,1,2,0:T(8,128)(2,1)S(1)}, bf16[51,16,3,128]{3,1,2,0:T(8,128)(2,1)S(1)}, u32[]{:S(2)}, u32[]{:S(2)}) collective-permute-start(bf16[51,16,3,128]{3,1,2,0:T(8,128)(2,1)S(1)} %copy.37), channel_id=1, source_target_pairs={{2,0},{4,2},{6,4},{8,6},{10,8},{12,10},{14,12},{16,14},{18,16},{20... | collective-permute-start | bytes 1880072 | tf_op jit(solution)/shard_map/ppermute | solution.py:24
  52.0 1.0 scatter_custom_fusion.1
  53.0 1.2 copy.33
  54.2 0.1 copy.34
  54.3 0.7 collective-permute-start
  55.0 0.1 fusion.54
  55.1 0.3 collective-permute-start.3
  55.4 1.4 %collective-permute-start.1 = (s32[51]{0:T(128)S(1)}, s32[51]{0:T(128)S(1)}, u32[]{:S(2)}, u32[]{:S(2)}) collective-permute-start(s32[51]{0:T(128)S(1)} %get-tuple-element.17), channel_id=1, source_target_pairs={{4,0},{6,2},{8,4},{10,6},{12,8},{14,10},{16,12},{18,14},{20,16},{2... | collective-permute-start | bytes 620 | tf_op jit(solution)/shard_map/ppermute | solution.py:24
  56.8 0.2 copy.39
  57.0 0.1 copy.40
  57.2 0.2 copy.32
  57.3 0.5 fusion.32
  57.8 0.2 copy.42
  58.0 0.1 copy.43
  58.1 15.2 %collective-permute-done.3 = s32[51]{0:T(128)S(1)} collective-permute-done((s32[51]{0:T(128)S(1)}, s32[51]{0:T(128)S(1)}, u32[]{:S(2)}, u32[]{:S(2)}) %collective-permute-start.3) | collective-permute-done | bytes 236 | tf_op jit(solution)/shard_map/ppermute | solution.py:24
  73.3 4.8 %collective-permute-start.5 = (s32[51]{0:T(128)S(1)}, s32[51]{0:T(128)S(1)}, u32[]{:S(2)}, u32[]{:S(2)}) collective-permute-start(s32[51]{0:T(128)S(1)} %get-tuple-element.15), channel_id=1, source_target_pairs={{30,0},{0,2},{2,4},{4,6},{6,8},{8,10},{10,12},{12,14},{14,16},{16,... | collective-permute-start | bytes 620 | tf_op jit(solution)/shard_map/ppermute | solution.py:24
  78.1 0.5 fusion.19
  78.6 3.1 %collective-permute-start.7 = (s32[51]{0:T(128)S(1)}, s32[51]{0:T(128)S(1)}, u32[]{:S(2)}, u32[]{:S(2)}) collective-permute-start(s32[51]{0:T(128)S(1)} %get-tuple-element.14), channel_id=1, source_target_pairs={{28,0},{30,2},{0,4},{2,6},{4,8},{6,10},{8,12},{10,14},{12,16},{14,... | collective-permute-start | bytes 620 | tf_op jit(solution)/shard_map/ppermute | solution.py:24
  81.7 0.5 fusion.21
  82.2 0.5 fusion.17
  82.7 14.2 %collective-permute-done.7 = s32[51]{0:T(128)S(1)} collective-permute-done((s32[51]{0:T(128)S(1)}, s32[51]{0:T(128)S(1)}, u32[]{:S(2)}, u32[]{:S(2)}) %collective-permute-start.7) | collective-permute-done | bytes 236 | tf_op jit(solution)/shard_map/ppermute | solution.py:24
  96.9 1.9 %add_bitcast_fusion = f32[16,3,64,128]{3,2,1,0:T(8,128)} fusion(f32[16,3,128,64]{2,3,1,0:T(8,128)S(1)} %fusion.17, f32[16,3,128,64]{2,3,1,0:T(8,128)S(1)} %fusion.19, f32[16,3,128,64]{2,3,1,0:T(8,128)S(1)} %fusion.32, f32[16,3,128,64]{2,3,1,0:T(8,128)S(1)} %fusion.21, bf16[51,16,3,128]{3,1,2,0:T(8,128)(2,1)S(1)} %collective-permute-done.6, ...), kind=kOutput, calls=%fused_computation.17 | convolution fusion | flops 41684160 | bytes 8491212 | tf_op jit(solution)/shard_map/rq,rlcb->lcqb/dot_general | solution.py:34
  98.7 25.3 %reduce-scatter.2.cloned.1.call-done = f32[8,3,64,128]{3,2,1,0:T(8,128)} async-done(((f32[16,3,64,128]{3,2,1,0:T(8,128)}), f32[8,3,64,128]{3,2,1,0:T(8,128)}) %reduce-scatter.2.cloned.1.call-update) | async-done | bytes 786448 | tf_op jit(solution)/shard_map/reduce_scatter | solution.py:95
  124.0 1.0 fusion.25
  125.0 1.0 compare_bitcast_fusion
  126.0 1.1 fusion.26
  127.2 0.9 copy.45
  (24 shorter events, 0.3 us)
Async XLA Ops:
  8.1 15.9 %all-to-all-start = ((bf16[2,2,8,2048]{3,2,1,0:T(8,128)(2,1)}), bf16[2,2,8,2048]{3,2,1,0:T(8,128)(2,1)S(1)}, u32[]{:S(2)}, u32[]{:S(2)}) async-start(bf16[2,2,8,2048]{3,2,1,0:T(8,128)(2,1)} %pad_maximum_fusion.1), calls=%async_computation | async-start | bytes 262144 | tf_op jit(solution)/shard_map/all_to_all | solution.py:14
  12.3 111.7 %reduce-scatter.2.cloned.1.call-start = ((), (), s32[]{:S(2)}) async-start(), calls=%async_computation.2 | async-start | bytes 2359296 | tf_op jit(solution)/shard_map/reduce_scatter | solution.py:95
  47.1 9.7 %copy-start.2 = (bf16[51,48,128]{2,1,0:T(8,128)(2,1)S(1)}, bf16[51,48,128]{2,1,0:T(8,128)(2,1)}, u32[]{:S(2)}) copy-start(bf16[51,48,128]{2,1,0:T(8,128)(2,1)} %get-tuple-element.8) | copy-start | bytes 1880068
  47.3 9.9 %copy-start.1 = (bf16[51,48,128]{2,1,0:T(8,128)(2,1)S(1)}, bf16[51,48,128]{2,1,0:T(8,128)(2,1)}, u32[]{:S(2)}) copy-start(bf16[51,48,128]{2,1,0:T(8,128)(2,1)} %get-tuple-element.11) | copy-start | bytes 1880068
  47.4 30.7 %collective-permute-start.2 = (bf16[51,16,3,128]{3,1,2,0:T(8,128)(2,1)S(1)}, bf16[51,16,3,128]{3,1,2,0:T(8,128)(2,1)S(1)}, u32[]{:S(2)}, u32[]{:S(2)}) collective-permute-start(bf16[51,16,3,128]{3,1,2,0:T(8,128)(2,1)S(1)} %copy.37), channel_id=1, source_target_pairs={{2,0},{4,2},{6,4},{8,6},{10,8},{12,10},{14,12},{16,14},{18,16},{20... | collective-permute-start | bytes 1880072 | tf_op jit(solution)/shard_map/ppermute | solution.py:24
  54.3 3.5 %copy-start = (bf16[51,48,128]{2,1,0:T(8,128)(2,1)S(1)}, bf16[51,48,128]{2,1,0:T(8,128)(2,1)}, u32[]{:S(2)}) copy-start(bf16[51,48,128]{2,1,0:T(8,128)(2,1)} %get-tuple-element.7) | copy-start | bytes 1880068
  54.3 27.4 %collective-permute-start = (bf16[51,16,3,128]{3,1,2,0:T(8,128)(2,1)S(1)}, bf16[51,16,3,128]{3,1,2,0:T(8,128)(2,1)S(1)}, u32[]{:S(2)}, u32[]{:S(2)}) collective-permute-start(bf16[51,16,3,128]{3,1,2,0:T(8,128)(2,1)S(1)} %copy.34), channel_id=1, source_target_pairs={{4,0},{6,2},{8,4},{10,6},{12,8},{14,10},{16,12},{18,14},{20,16},{2... | collective-permute-start | bytes 1880072 | tf_op jit(solution)/shard_map/ppermute | solution.py:24
  55.1 18.2 %collective-permute-start.3 = (s32[51]{0:T(128)S(1)}, s32[51]{0:T(128)S(1)}, u32[]{:S(2)}, u32[]{:S(2)}) collective-permute-start(s32[51]{0:T(128)S(1)} %get-tuple-element.16), channel_id=1, source_target_pairs={{2,0},{4,2},{6,4},{8,6},{10,8},{12,10},{14,12},{16,14},{18,16},{20... | collective-permute-start | bytes 620 | tf_op jit(solution)/shard_map/ppermute | solution.py:24
  55.4 23.1 %collective-permute-start.1 = (s32[51]{0:T(128)S(1)}, s32[51]{0:T(128)S(1)}, u32[]{:S(2)}, u32[]{:S(2)}) collective-permute-start(s32[51]{0:T(128)S(1)} %get-tuple-element.17), channel_id=1, source_target_pairs={{4,0},{6,2},{8,4},{10,6},{12,8},{14,10},{16,12},{18,14},{20,16},{2... | collective-permute-start | bytes 620 | tf_op jit(solution)/shard_map/ppermute | solution.py:24
  57.1 25.1 %collective-permute-start.4 = (bf16[51,16,3,128]{3,1,2,0:T(8,128)(2,1)S(1)}, bf16[51,16,3,128]{3,1,2,0:T(8,128)(2,1)S(1)}, u32[]{:S(2)}, u32[]{:S(2)}) collective-permute-start(bf16[51,16,3,128]{3,1,2,0:T(8,128)(2,1)S(1)} %copy.40), channel_id=1, source_target_pairs={{30,0},{0,2},{2,4},{4,6},{6,8},{8,10},{10,12},{12,14},{14,16},{16,... | collective-permute-start | bytes 1880072 | tf_op jit(solution)/shard_map/ppermute | solution.py:24
  73.3 8.9 %collective-permute-start.5 = (s32[51]{0:T(128)S(1)}, s32[51]{0:T(128)S(1)}, u32[]{:S(2)}, u32[]{:S(2)}) collective-permute-start(s32[51]{0:T(128)S(1)} %get-tuple-element.15), channel_id=1, source_target_pairs={{30,0},{0,2},{2,4},{4,6},{6,8},{8,10},{10,12},{12,14},{14,16},{16,... | collective-permute-start | bytes 620 | tf_op jit(solution)/shard_map/ppermute | solution.py:24
  78.1 18.8 %collective-permute-start.6 = (bf16[51,16,3,128]{3,1,2,0:T(8,128)(2,1)S(1)}, bf16[51,16,3,128]{3,1,2,0:T(8,128)(2,1)S(1)}, u32[]{:S(2)}, u32[]{:S(2)}) collective-permute-start(bf16[51,16,3,128]{3,1,2,0:T(8,128)(2,1)S(1)} %copy.43), channel_id=1, source_target_pairs={{28,0},{30,2},{0,4},{2,6},{4,8},{6,10},{8,12},{10,14},{12,16},{14,... | collective-permute-start | bytes 1880072 | tf_op jit(solution)/shard_map/ppermute | solution.py:24
  78.6 18.3 %collective-permute-start.7 = (s32[51]{0:T(128)S(1)}, s32[51]{0:T(128)S(1)}, u32[]{:S(2)}, u32[]{:S(2)}) collective-permute-start(s32[51]{0:T(128)S(1)} %get-tuple-element.14), channel_id=1, source_target_pairs={{28,0},{30,2},{0,4},{2,6},{4,8},{6,10},{8,12},{10,14},{12,16},{14,... | collective-permute-start | bytes 620 | tf_op jit(solution)/shard_map/ppermute | solution.py:24
Sparse Core Ops, SparseCore 0:
  98.9 25.1 reduce-scatter.1
